TPU v7x, 32 devices: a whole 2x2x4 slice. The times are simulated.
32 devices in a mesh: pts: 8 (over y, x, core), freq: 4 (over z).
Axes of the slice: x: 2, y: 2, z: 4, core: 2. Of those that a mesh axis runs over, the one named last changes fastest.
Arguments:
- spectra: bfloat16 [128, 2, 32, 16384], P('freq', None, None, 'pts'), may hold values from -6 to 6
- weights: float32 [16384], P('pts'), may hold values from 0.25 to 4
- triads: int32 [64, 2], replicated, may hold values from 0 to 127, as said below
Outputs:
- bispectrum: float32 [64, 2, 32, 32], P('freq')
- density: float32 [128, 2, 32, 32], P('freq')
- vectors: float32 [64, 2, 32], P('freq')
- energy: float32 [64], P('freq')
- mode_fields: float32 [64, 2, 16384], P('freq', None, 'pts')
Inputs may be any that keep to these rules, and one draw needn't show every extreme that they name: Row t holds (k, l) of triad t. The triads of group g, rows g * 16 to (g + 1) * 16 - 1, have k within the group's own frequencies g * 32 to (g + 1) * 32 - 1. The l of exactly 4 triads of each group lie in each group's frequency range. Among the 32 frequencies l and (k + l) mod 128 of one group's triads, at most 12 lie in any one group's range, and in every group some range holds exactly 12.
All inputs are finite; a program needn't handle non-finite values.
Results may differ from a plain program's by a relative error of at most 0.0052.
Values may be sent and summed in bfloat16 or wider, within the bound.
A program may use at most 128 MiB of HBM per device.

v0:
```python
import math

import jax
import jax.numpy as jnp
from jax import lax
from jax.sharding import PartitionSpec as P

ITERS = 3


highest = lax.Precision.HIGHEST


def block_gram(left, right):
    half_rows = left.shape[2]
    lead_dims = left.shape[:1]
    flat_left = left.reshape(lead_dims + (2 * half_rows, left.shape[3]))
    flat_right = right.reshape(lead_dims + (2 * half_rows, right.shape[3]))
    joined = jnp.einsum("tap,tbp->tab", flat_left, flat_right, preferred_element_type=jnp.float32)
    real_part = joined[:, :half_rows, :half_rows] + joined[:, half_rows:, half_rows:]
    imag_part = joined[:, :half_rows, half_rows:] - joined[:, half_rows:, :half_rows]
    return jnp.stack([real_part, imag_part], axis=1)


def weighted_product(first_rows, second_rows, weights):
    first_real = first_rows[:, 0].astype(jnp.float32)
    first_imag = first_rows[:, 1].astype(jnp.float32)
    second_real = second_rows[:, 0].astype(jnp.float32)
    second_imag = second_rows[:, 1].astype(jnp.float32)
    prod_real = first_real * second_real - first_imag * second_imag
    prod_imag = first_real * second_imag + first_imag * second_real
    return (jnp.stack([prod_real, prod_imag], axis=1) * weights).astype(jnp.bfloat16)


def apply_matrix(matrix, vector):
    return jnp.einsum("...ab,...b->...a", matrix, vector, precision=highest)


def apply_adjoint(matrix, vector):
    return jnp.einsum("...ba,...b->...a", matrix, vector, precision=highest)


def power_iteration(bispec):
    real_mat = bispec[..., 0, :, :]
    imag_mat = bispec[..., 1, :, :]
    order = real_mat.shape[-1]
    vec_real = jnp.full(real_mat.shape[:-1], 1.0 / math.sqrt(order), jnp.float32)
    vec_imag = jnp.zeros(real_mat.shape[:-1], jnp.float32)
    for sweep_index in range(ITERS):
        out_real = apply_matrix(real_mat, vec_real) - apply_matrix(imag_mat, vec_imag)
        out_imag = apply_matrix(real_mat, vec_imag) + apply_matrix(imag_mat, vec_real)
        back_real = apply_adjoint(real_mat, out_real) + apply_adjoint(imag_mat, out_imag)
        back_imag = apply_adjoint(real_mat, out_imag) - apply_adjoint(imag_mat, out_real)
        factor = 1.0 / jnp.sqrt(
            jnp.sum(back_real * back_real + back_imag * back_imag, axis=-1) + 1.0
        )
        vec_real = back_real * factor[..., None]
        vec_imag = back_imag * factor[..., None]
    out_real = apply_matrix(real_mat, vec_real) - apply_matrix(imag_mat, vec_imag)
    out_imag = apply_matrix(real_mat, vec_imag) + apply_matrix(imag_mat, vec_real)
    top_part = jnp.sum(out_real * out_real + out_imag * out_imag, axis=-1)
    bottom_part = order * (jnp.sum(vec_real * vec_real + vec_imag * vec_imag, axis=-1) + 1.0)
    return (jnp.stack([vec_real, vec_imag], axis=-2), top_part / bottom_part)


def fetch_slots(spectra, triads, group_index, freq_count, f_dev, per_group):
    freq_total = f_dev * freq_count
    cap_rows = 3 * per_group // freq_count
    need_count = 2 * per_group
    freq_first = triads[:, 0]
    freq_second = triads[:, 1]
    wanted = jnp.stack([freq_second, (freq_first + freq_second) % freq_total], axis=1).reshape(
        freq_count, need_count
    )
    owners = wanted // f_dev
    earlier = lax.broadcasted_iota(jnp.int32, (need_count, need_count), 1) < lax.broadcasted_iota(
        jnp.int32, (need_count, need_count), 0
    )
    same_owner = owners[:, :, None] == owners[:, None, :]
    slot_rank = jnp.sum(jnp.where(same_owner & earlier[None], 1, 0), axis=2).astype(jnp.int32)
    slot_ids = lax.broadcasted_iota(jnp.int32, (1, cap_rows, 1), 1)
    chosen = (owners[:, None, :] == group_index) & (slot_rank[:, None, :] == slot_ids)
    local_row = wanted - group_index * f_dev
    row_index = jnp.sum(jnp.where(chosen, local_row[:, None, :], 0), axis=2)
    outgoing = jnp.take(spectra, row_index.reshape(-1), axis=0).reshape(
        (freq_count, cap_rows) + spectra.shape[1:]
    )
    incoming = lax.all_to_all(outgoing, "freq", split_axis=0, concat_axis=0, tiled=True)
    flat_rows = incoming.reshape((freq_count * cap_rows,) + spectra.shape[1:])
    own_owner = lax.dynamic_index_in_dim(owners, group_index, 0, keepdims=False)
    own_slot = lax.dynamic_index_in_dim(slot_rank, group_index, 0, keepdims=False)
    picked = jnp.take(flat_rows, own_owner * cap_rows + own_slot, axis=0)
    return (picked[0::2], picked[1::2])


def local(spectra, weights, triads):
    freq_count = lax.axis_size("freq")
    group_index = lax.axis_index("freq")
    f_dev = spectra.shape[0]
    blocks = spectra.shape[2]
    per_group = triads.shape[0] // freq_count
    point_count = spectra.shape[3] * lax.axis_size("pts")
    own_triads = lax.dynamic_slice_in_dim(triads, group_index * per_group, per_group, 0)
    k_mine = own_triads[:, 0]
    first_rows = jnp.take(spectra, k_mine - group_index * f_dev, axis=0)
    second_rows, third_rows = fetch_slots(
        spectra, triads, group_index, freq_count, f_dev, per_group
    )
    weighted_spectra = (spectra.astype(jnp.float32) * weights).astype(jnp.bfloat16)
    density_part = block_gram(weighted_spectra, spectra)
    bis_part = block_gram(weighted_product(first_rows, second_rows, weights), third_rows)
    bis_scale = 1.0 / math.sqrt(blocks * point_count)
    dens_scale = 1.0 / point_count
    bis_total, dens_total = lax.psum((bis_part, density_part), "pts")
    bispectrum = bis_total * bis_scale
    density = dens_total * dens_scale
    vectors, energy = power_iteration(bispectrum)
    vector_low = vectors.astype(jnp.bfloat16)
    mixed = jnp.einsum("tcbp,tdb->tcdp", third_rows, vector_low, preferred_element_type=jnp.float32)
    mode_fields = jnp.stack(
        [mixed[:, 0, 0] - mixed[:, 1, 1], mixed[:, 0, 1] + mixed[:, 1, 0]], axis=1
    )
    return (bispectrum, density, vectors, energy, mode_fields)


def solution(mesh):
    in_specs = (P("freq", None, None, "pts"), P("pts"), P())
    out_specs = (
        P("freq", None, None, None),
        P("freq", None, None, None),
        P("freq", None, None),
        P("freq"),
        P("freq", None, "pts"),
    )
    return jax.shard_map(local, mesh=mesh, in_specs=in_specs, out_specs=out_specs, check_vma=False)
```

profile of v0, /device:TPU:0, one launch (start us, length us, event | category | flops | bytes accessed | tf_op | source)
XLA Modules:
  0.0 425.3 jit_solution(13163111517294310016)
XLA Ops:
  9.0 9.7 %gather_fusion.1 = bf16[48,2,32,2048]{3,2,1,0:T(8,128)(2,1)} fusion(bf16[32,2,32,2048]{3,2,1,0:T(8,128)(2,1)} %param.3, s32[1024]{0:T(1024)S(1)} %pad_clamp_fusion.1), kind=kCustom, calls=%fused_computation.1 | custom fusion | bytes 25166016 | tf_op jit(solution)/shard_map/jit(_take)/gather | solution.py:85
  18.7 10.9 %broadcast_select_fusion = bf16[4,12,2,32,2048]{4,3,2,1,0:T(8,128)(2,1)} fusion(bf16[4,12,2,32,2048]{4,3,2,1,0:T(8,128)(2,1)} %bitcast.212, pred[4,12]{1,0:T(4,128)(4,1)S(1)} %copy.21), kind=kLoop, calls=%fused_computation.4 | loop fusion | flops 6291456 | bytes 25165872 | tf_op jit(solution)/shard_map/jit(_take)/select_n | solution.py:85
  29.6 6.5 %all-to-all-start = ((bf16[4,12,2,32,2048]{4,3,2,1,0:T(8,128)(2,1)}), bf16[4,12,2,32,2048]{4,3,2,1,0:T(8,128)(2,1)}, u32[]{:S(2)}, u32[]{:S(2)}) async-start(bf16[4,12,2,32,2048]{4,3,2,1,0:T(8,128)(2,1)} %broadcast_select_fusion), calls=%async_computation | async-start | bytes 25165824 | tf_op jit(solution)/shard_map/all_to_all | solution.py:88
  36.2 6.2 %gather_fusion = bf16[16,2,32,2048]{3,2,1,0:T(8,128)(2,1)} fusion(bf16[32,2,32,2048]{3,2,1,0:T(8,128)(2,1)} %param.3, s32[1024]{0:T(1024)S(1)} %pad_clamp_fusion.2), kind=kCustom, calls=%fused_computation | custom fusion | bytes 8388672 | tf_op jit(solution)/shard_map/jit(_take)/gather | solution.py:105
  42.5 9.7 %multiply_convert_fusion = bf16[32,2,32,2048]{3,2,1,0:T(8,128)(2,1)} fusion(bf16[32,2,32,2048]{3,2,1,0:T(8,128)(2,1)} %param.3, f32[2048]{0:T(1024)S(1)} %copy-done.4), kind=kLoop, calls=%fused_computation.3 | loop fusion | flops 12582912 | bytes 16785408 | tf_op jit(solution)/shard_map/convert_element_type | solution.py:109
  52.2 8.1 %fusion.53 = f32[32,64,64]{2,1,0:T(8,128)S(1)} fusion(bf16[32,64,2048]{2,1,0:T(8,128)(2,1)} %bitcast.213, bf16[32,64,2048]{2,1,0:T(8,128)(2,1)} %bitcast.211), kind=kOutput, calls=%fused_computation.125 | convolution fusion | flops 536870912 | bytes 17301504 | tf_op jit(solution)/shard_map/tap,tbp->tab/dot_general | solution.py:19
  60.6 1.1 pad_maximum_fusion.1
  61.7 1.2 copy-done
  62.8 2.4 broadcast_select_fusion.2
  65.3 245.5 %all-to-all-done = bf16[4,12,2,32,2048]{4,3,2,1,0:T(8,128)(2,1)} async-done(((bf16[4,12,2,32,2048]{4,3,2,1,0:T(8,128)(2,1)}), bf16[4,12,2,32,2048]{4,3,2,1,0:T(8,128)(2,1)}, u32[]{:S(2)}, u32[]{:S(2)}) %all-to-all-start) | async-done | bytes 12582944 | tf_op jit(solution)/shard_map/all_to_all | solution.py:88
  310.7 9.6 %gather_fusion.2 = bf16[32,2,32,2048]{3,2,1,0:T(8,128)(2,1)} fusion(bf16[48,2,32,2048]{3,2,1,0:T(8,128)(2,1)} %bitcast.5, s32[1024]{0:T(1024)S(1)} %pad_clamp_fusion), kind=kCustom, calls=%fused_computation.2 | custom fusion | bytes 16777344 | tf_op jit(solution)/shard_map/jit(_take)/gather | solution.py:92
  320.3 7.5 %broadcast_select_fusion.1 = bf16[32,2,32,2048]{3,2,1,0:T(8,128)(2,1)} fusion(bf16[32,2,32,2048]{3,2,1,0:T(8,128)(2,1)} %gather_fusion.2, pred[32]{0:T(512)(128)(4,1)S(1)} %get-tuple-element.36), kind=kLoop, calls=%fused_computation.8 | loop fusion | flops 4194304 | bytes 16777248 | tf_op jit(solution)/shard_map/jit(_take)/select_n | solution.py:92
  327.7 4.0 fusion.50
  332.4 1.9 fusion.1
  334.3 1.1 pad_maximum_fusion
  335.4 1.3 fusion
  336.7 1.2 fusion.52
  338.1 0.8 pad_maximum_fusion.2
  339.0 58.1 %all-reduce.3.cloned.1.call-done = (f32[16,2,32,32]{3,2,0,1:T(8,128)}, f32[32,2,32,32]{3,2,0,1:T(8,128)}) async-done(((f32[16,2,32,32]{3,2,0,1:T(8,128)}, f32[32,2,32,32]{3,2,0,1:T(8,128)}), (f32[16,2,32,32]{3,2,0,1:T(8,128)}, f32[32,2,32,32]{3,2,0,1:T(8,128)})) %all-reduce.3.cloned.1.call-update) | async-done | bytes 393232 | tf_op jit(solution)/shard_map/psum | solution.py:114
  397.0 1.1 broadcast_multiply_fusion.1
  409.5 2.9 convolution_bitcast_fusion
  414.9 0.8 copy.26
  415.8 1.1 copy.27
  416.9 0.9 pad_maximum_fusion.3
  (87 shorter events, 17.6 us)
Async XLA Ops:
  29.6 6.5 %copy-start.5 = (s32[64,2]{0,1:T(2,128)S(1)}, s32[64,2]{0,1:T(2,128)}, u32[]{:S(2)}) copy-start(s32[64,2]{0,1:T(2,128)} %param.5) | copy-start | bytes 1540
  29.6 281.1 %all-to-all-start = ((bf16[4,12,2,32,2048]{4,3,2,1,0:T(8,128)(2,1)}), bf16[4,12,2,32,2048]{4,3,2,1,0:T(8,128)(2,1)}, u32[]{:S(2)}, u32[]{:S(2)}) async-start(bf16[4,12,2,32,2048]{4,3,2,1,0:T(8,128)(2,1)} %broadcast_select_fusion), calls=%async_computation | async-start | bytes 25165824 | tf_op jit(solution)/shard_map/all_to_all | solution.py:88
  36.1 6.4 %copy-start.4 = (f32[2048]{0:T(1024)S(1)}, f32[2048]{0:T(1024)}, u32[]{:S(2)}) copy-start(f32[2048]{0:T(1024)} %param.4) | copy-start | bytes 24580
  36.1 361.0 %all-reduce.3.cloned.1.call-start = ((), (), s32[]{:S(2)}) async-start(), calls=%async_computation.1 | async-start | bytes 3145728 | tf_op jit(solution)/shard_map/psum | solution.py:114
  60.3 2.6 copy-start
  327.7 4.7 %copy-start.1 = (bf16[16,2,32,2048]{3,2,1,0:T(8,128)(2,1)S(1)}, bf16[16,2,32,2048]{3,2,1,0:T(8,128)(2,1)}, u32[]{:S(2)}) copy-start(bf16[16,2,32,2048]{3,2,1,0:T(8,128)(2,1)} %broadcast_select_fusion.2) | copy-start | bytes 12582916
  401.8 13.9 %copy-start.2 = (f32[32,2,32,32]{3,2,0,1:T(8,128)S(1)}, f32[32,2,32,32]{3,2,0,1:T(8,128)}, u32[]{:S(2)}) copy-start(f32[32,2,32,32]{3,2,0,1:T(8,128)} %get-tuple-element.21) | copy-start | bytes 786436
  409.5 9.0 %copy-start.3 = (f32[16,2,32]{2,1,0:T(2,128)}, f32[16,2,32]{2,1,0:T(2,128)S(1)}, u32[]{:S(2)}) copy-start(f32[16,2,32]{2,1,0:T(2,128)S(1)} %pad_maximum_fusion.4) | copy-start | bytes 12292
Sparse Core Ops, SparseCore 0:
  339.1 57.9 all-reduce.2
where the time goes:
time: 426 us; the launch traced here: 425 us
  waiting for transfers between devices  304 us (71%)
  other arithmetic  42.4 us (10%)
  local copies, waits for them, and re-layouts  33.8 us (8%)
  matrix products  24.8 us (6%)
  between operations  14.3 us (3%)
  starting transfers between devices  6.52 us (2%)
    all_to_all x1, waiting for transfers between devices, fetch_slots(): lax.all_to_all(outgoing, 'freq', split_axis=0, concat_axis=0, tiled=True)  245 us
    psum x1, waiting for transfers between devices, local(): bis_total, dens_total = lax.psum((bis_part, density_part), 'pts')  58.1 us
    select_n x2, other arithmetic, fetch_slots(): jnp.take(spectra, row_index.reshape(-1), axis=0)  10.9 us
    convert_element_type x1, other arithmetic, local(): (spectra.astype(jnp.float32) * weights).astype(jnp.bfloat16)  9.7 us
    gather x1, local copies, waits for them, and re-layouts, fetch_slots(): jnp.take(spectra, row_index.reshape(-1), axis=0)  9.69 us
    gather x1, local copies, waits for them, and re-layouts, fetch_slots(): picked = jnp.take(flat_rows, own_owner * cap_rows + own_slot, axis=0)  9.58 us
    dot_general x2, matrix products, block_gram(): jnp.einsum('tap,tbp->tab', flat_left, flat_right, preferred_element_type=...  9.33 us
  transfers between devices with their start and end apart: 2, of which 2 were waited for; matrix products, arithmetic and copies ran while one was open for 7% of the time, Pallas kernels for 0%

commit v1 on v0

v1 whole, which is shorter than its diff:
```python
import functools
import math

import jax
import jax.numpy as jnp
from jax import lax
from jax.experimental import pallas as pl
from jax.experimental.pallas import tpu as pltpu
from jax.sharding import PartitionSpec as P

ITERS = 3
MESH = pl.DeviceIdType.MESH
f32 = jnp.float32
bf16 = jnp.bfloat16


def gram_pair(left_real, left_imag, right_real, right_imag):
    left = jnp.concatenate([left_real, left_imag], axis=1)
    right = jnp.concatenate(
        [
            jnp.concatenate([right_real, right_imag], axis=1),
            jnp.concatenate([right_imag, -right_real], axis=1),
        ],
        axis=0,
    )
    return lax.dot_general(left, right, (((1,), (1,)), ((), ())), preferred_element_type=f32)


def lane_in(shape):
    return lax.broadcasted_iota(jnp.int32, shape, len(shape) - 1)


def segment_sum(values, low):
    first = jnp.sum(jnp.where(low, values, 0.0), axis=-1, keepdims=True)
    second = jnp.sum(jnp.where(low, 0.0, values), axis=-1, keepdims=True)
    return first, second


def swap_parts(values, is_real):
    axis = values.ndim - 1
    up = pltpu.roll(values, 96, axis)
    down = pltpu.roll(values, 32, axis)
    return jnp.where(is_real, up, down)


def kernel(
    groups,
    point_devs,
    chunks,
    tri_ref,
    w_ref,
    spec_ref,
    bis_out,
    dens_out,
    vec_out,
    energy_out,
    mode_out,
    own,
    acc,
    r1,
    s1,
    r2,
    fin,
    full,
    dacc,
    rd,
    dfin,
    dfull,
    lhs_mine,
    lhs_all,
    modes,
    mode_buf,
    own_sem,
    loc_sem,
    main_send,
    main_recv,
    d1_send,
    d1_recv,
    d2_send,
    d2_recv,
    r1_send,
    r1_recv,
    r2_send,
    r2_recv,
    r3_send,
    r3_recv,
    l_send,
    l_recv,
    m_send,
    m_recv,
    *bufs,
):
    z = lax.axis_index("freq")
    q = lax.axis_index("pts")
    f_dev, _, blocks, points = spec_ref.shape
    width = points // groups
    cw = width // chunks
    triads = tri_ref.shape[0]
    f_total = f_dev * groups
    per_group = triads // groups
    pairs_g = per_group // 2
    tpd = fin.shape[0]
    td = dfin.shape[0]
    zs = [lax.rem(z + s, groups) for s in range(1, groups)]
    zr = [lax.rem(z + groups - s, groups) for s in range(1, groups)]
    qs = [lax.rem(q + s, point_devs) for s in range(1, point_devs)]
    qr = [lax.rem(q + point_devs - s, point_devs) for s in range(1, point_devs)]

    barrier = pltpu.get_barrier_semaphore()
    for j in zs:
        pl.semaphore_signal(barrier, inc=1, device_id={"freq": j}, device_id_type=MESH)
    for j in qs:
        pl.semaphore_signal(barrier, inc=1, device_id={"pts": j}, device_id_type=MESH)
    pl.semaphore_wait(barrier, groups - 1 + point_devs - 1)

    def piece(owner, c):
        start = pl.multiple_of(owner * width + c * cw, 128)
        return spec_ref.at[:, :, :, pl.ds(start, cw)]

    def remote(src, dst, send, recv, axis, j):
        return pltpu.make_async_remote_copy(
            src_ref=src,
            dst_ref=dst,
            send_sem=send,
            recv_sem=recv,
            device_id={axis: j},
            device_id_type=MESH,
        )

    sends = []
    main = [[None] * (groups - 1) for _ in range(chunks)]
    for c in range(chunks):
        for s in range(groups - 1):
            copy = remote(
                piece(zs[s], c),
                bufs[c].at[pl.ds(z * f_dev, f_dev)],
                main_send.at[c, s],
                main_recv.at[c, s],
                "freq",
                zs[s],
            )
            copy.start()
            main[c][s] = copy
    own_copy = pltpu.make_async_copy(spec_ref, own, own_sem)
    own_copy.start()
    local_copies = []
    for c in range(chunks):
        copy = pltpu.make_async_copy(
            piece(z, c), bufs[c].at[pl.ds(z * f_dev, f_dev)], loc_sem.at[c]
        )
        copy.start()
        local_copies.append(copy)
    own_copy.wait()

    weights_row = w_ref[...]

    def density_body(i, carry):
        halves = []
        for h in range(2):
            rows = own[2 * i + h]
            real, imag = rows[0], rows[1]
            wr = (real.astype(f32) * weights_row).astype(bf16)
            wi = (imag.astype(f32) * weights_row).astype(bf16)
            halves.append(gram_pair(wr, wi, real, imag))
        out = jnp.concatenate(halves, axis=1) * (1.0 / (points * point_devs))
        dacc[pl.ds(i * 4, 4)] = out.reshape(4, 8, 128)
        return carry

    lax.fori_loop(0, f_dev // 2, density_body, 0)

    copies = []
    for s in range(point_devs - 1):
        copy = remote(
            dacc.at[pl.ds(qs[s] * td, td)], rd.at[s], d1_send.at[s], d1_recv.at[s], "pts", qs[s]
        )
        copy.start()
        copies.append(copy)
    for copy in copies:
        copy.wait()
    total = dacc[pl.ds(q * td, td)]
    for s in range(point_devs - 1):
        total = total + rd[s]
    dfin[...] = total
    dfull[pl.ds(q * td, td)] = total
    dens_gather = []
    for s in range(point_devs - 1):
        copy = remote(
            dfin, dfull.at[pl.ds(q * td, td)], d2_send.at[s], d2_recv.at[s], "pts", qs[s]
        )
        copy.start()
        dens_gather.append(copy)

    bis_scale = 1.0 / math.sqrt(blocks * points * point_devs)

    for c in range(chunks):
        local_copies[c].wait()
        for s in range(groups - 1):
            pltpu.make_async_copy(
                bufs[c].at[pl.ds(zr[s] * f_dev, f_dev)],
                bufs[c].at[pl.ds(zr[s] * f_dev, f_dev)],
                main_recv.at[c, s],
            ).wait()
        w_piece = w_ref[:, pl.ds(pl.multiple_of(z * width + c * cw, 128), cw)]
        buf = bufs[c]

        def triad_body(i, carry):
            halves = []
            for h in range(2):
                t = 2 * i + h
                k = tri_ref[t, 0]
                l = tri_ref[t, 1]
                m = jnp.where(k + l >= f_total, k + l - f_total, k + l)
                first = buf[k].astype(f32)
                second = buf[l].astype(f32)
                third = buf[m]
                pr = first[0] * second[0] - first[1] * second[1]
                pi = first[0] * second[1] + first[1] * second[0]
                pr = (pr * w_piece).astype(bf16)
                pi = (pi * w_piece).astype(bf16)
                halves.append(gram_pair(pr, pi, third[0], third[1]))
            out = jnp.concatenate(halves, axis=1).reshape(4, 8, 128)
            g = i // pairs_g
            at = (i - g * pairs_g) * 4
            if c == 0:
                acc[g, pl.ds(at, 4)] = out
            else:
                acc[g, pl.ds(at, 4)] += out
            return carry

        lax.fori_loop(0, triads // 2, triad_body, 0)

    copies = []
    for s in range(point_devs - 1):
        copy = remote(
            acc.at[:, pl.ds(qs[s] * tpd, tpd)], r1.at[s], r1_send.at[s], r1_recv.at[s], "pts", qs[s]
        )
        copy.start()
        copies.append(copy)
    for copy in dens_gather:
        copy.wait()
    dens_out[...] = dfull[...]
    for copy in copies:
        copy.wait()
    total = acc[:, pl.ds(q * tpd, tpd)]
    for s in range(point_devs - 1):
        total = total + r1[s]
    s1[...] = total
    copies = []
    for s in range(groups - 1):
        copy = remote(s1.at[zs[s]], r2.at[s], r2_send.at[s], r2_recv.at[s], "freq", zs[s])
        copy.start()
        copies.append(copy)
    for copy in copies:
        copy.wait()
    total = s1[z]
    for s in range(groups - 1):
        total = total + r2[s]
    total = total * bis_scale
    fin[...] = total
    full[pl.ds(q * tpd, tpd)] = total
    copies = []
    for s in range(point_devs - 1):
        copy = remote(
            fin, full.at[pl.ds(q * tpd, tpd)], r3_send.at[s], r3_recv.at[s], "pts", qs[s]
        )
        copy.start()
        copies.append(copy)
    for copy in copies:
        copy.wait()
    bis_out[...] = full[...]
    mat = full[...].reshape(pairs_g, 32, 128)

    lane_m = lane_in((pairs_g, 32, 128))
    low_m = lane_m < 64
    lane_v = lane_in((pairs_g, 1, 128))
    low_v = lane_v < 64
    real_v = lax.rem(lane_v, 64) < 32

    def apply(vec):
        va = jnp.where(real_v, vec, -vec)
        vb = swap_parts(vec, real_v)
        re0, re1 = segment_sum(mat * va, low_m)
        im0, im1 = segment_sum(mat * vb, low_m)
        return jnp.where(low_m, re0, re1), jnp.where(low_m, im0, im1)

    vec = jnp.where(real_v, 1.0 / math.sqrt(blocks), 0.0)
    for _ in range(ITERS):
        ur, ui = apply(vec)
        x = jnp.sum(mat * ur, axis=1, keepdims=True)
        y = jnp.sum(mat * ui, axis=1, keepdims=True)
        ys = swap_parts(y, real_v)
        w = jnp.where(real_v, x + ys, ys - x)
        n0, n1 = segment_sum(w * w, low_v)
        vec = w * (1.0 / jnp.sqrt(jnp.where(low_v, n0, n1) + 1.0))
    ur, ui = apply(vec)
    top = jnp.sum(ur * ur + ui * ui, axis=1, keepdims=True)
    n0, n1 = segment_sum(vec * vec, low_v)
    energy_out[...] = top / (blocks * (jnp.where(low_v, n0, n1) + 1.0))
    vec_out[...] = vec

    va = jnp.where(real_v, vec, -vec)
    vb = swap_parts(vec, real_v)
    row = lax.broadcasted_iota(jnp.int32, (8, 256), 0)
    col = lax.broadcasted_iota(jnp.int32, (8, 256), 1)
    keep = (col // 64) == (row // 2)
    even = lax.rem(row, 2) == 0
    for j in range(per_group // 4):
        a = jnp.concatenate([va[2 * j], va[2 * j + 1]], axis=1)
        b = jnp.concatenate([vb[2 * j], vb[2 * j + 1]], axis=1)
        block = jnp.where(keep, jnp.where(even, a, b), 0.0)
        lhs_mine[j] = block
        lhs_all[z, j] = block
    copies = []
    for s in range(groups - 1):
        copy = remote(lhs_mine, lhs_all.at[z], l_send.at[s], l_recv.at[s], "freq", zs[s])
        copy.start()
        copies.append(copy)

    def mode_rows(g, j, c):
        parts = []
        for i in range(4):
            t = g * per_group + j * 4 + i
            k = tri_ref[t, 0]
            l = tri_ref[t, 1]
            m = jnp.where(k + l >= f_total, k + l - f_total, k + l)
            parts.append(bufs[c][m].reshape(2 * blocks, cw))
        right = jnp.concatenate(parts, axis=0)
        return jnp.dot(lhs_all[g, j].astype(bf16), right, preferred_element_type=f32)

    for copy in copies:
        copy.wait()
    copies = []
    for s in range(groups - 1):
        g = zs[s]

        def mode_body(j, carry, g=g):
            for c in range(chunks):
                modes[g, pl.ds(pl.multiple_of(j * 8, 8), 8), c * cw : (c + 1) * cw] = mode_rows(
                    g, j, c
                )
            return carry

        lax.fori_loop(0, per_group // 4, mode_body, 0)
        copy = remote(
            modes.at[g],
            mode_buf.at[:, pl.ds(pl.multiple_of(z * width, 128), width)],
            m_send.at[s],
            m_recv.at[s],
            "freq",
            g,
        )
        copy.start()
        copies.append(copy)

    def own_mode_body(j, carry):
        for c in range(chunks):
            mode_buf[
                pl.ds(pl.multiple_of(j * 8, 8), 8),
                pl.ds(pl.multiple_of(z * width + c * cw, 128), cw),
            ] = mode_rows(z, j, c)
        return carry

    lax.fori_loop(0, per_group // 4, own_mode_body, 0)
    for c in range(chunks):
        for s in range(groups - 1):
            main[c][s].wait_send()
    for copy in copies:
        copy.wait()
    mode_out[...] = mode_buf[...]


def local(spectra, weights, triads):
    groups = lax.axis_size("freq")
    point_devs = lax.axis_size("pts")
    f_dev, _, blocks, points = spectra.shape
    tri_count = triads.shape[0]
    per_group = tri_count // groups
    pairs_g = per_group // 2
    width = points // groups
    chunks = width // 128
    cw = width // chunks
    tpd = pairs_g * 4 // point_devs
    td = f_dev // 2 * 4 // point_devs
    vmem = pl.BlockSpec(memory_space=pltpu.VMEM)
    dma = pltpu.SemaphoreType.DMA
    z1, p1 = groups - 1, point_devs - 1
    outs = pl.pallas_call(
        functools.partial(kernel, groups, point_devs, chunks),
        out_shape=[
            jax.ShapeDtypeStruct((pairs_g * 4, 8, 128), f32),
            jax.ShapeDtypeStruct((f_dev * 2, 8, 128), f32),
            jax.ShapeDtypeStruct((pairs_g, 1, 128), f32),
            jax.ShapeDtypeStruct((pairs_g, 1, 128), f32),
            jax.ShapeDtypeStruct((2 * per_group, points), f32),
        ],
        in_specs=[
            pl.BlockSpec(memory_space=pltpu.SMEM),
            vmem,
            pl.BlockSpec(memory_space=pl.ANY),
        ],
        out_specs=[vmem] * 5,
        scratch_shapes=[
            pltpu.VMEM(spectra.shape, bf16),
            pltpu.VMEM((groups, pairs_g * 4, 8, 128), f32),
            pltpu.VMEM((p1, groups, tpd, 8, 128), f32),
            pltpu.VMEM((groups, tpd, 8, 128), f32),
            pltpu.VMEM((z1, tpd, 8, 128), f32),
            pltpu.VMEM((tpd, 8, 128), f32),
            pltpu.VMEM((pairs_g * 4, 8, 128), f32),
            pltpu.VMEM((f_dev * 2, 8, 128), f32),
            pltpu.VMEM((p1, td, 8, 128), f32),
            pltpu.VMEM((td, 8, 128), f32),
            pltpu.VMEM((f_dev * 2, 8, 128), f32),
            pltpu.VMEM((per_group // 4, 8, 256), f32),
            pltpu.VMEM((groups, per_group // 4, 8, 256), f32),
            pltpu.VMEM((groups, 2 * per_group, width), f32),
            pltpu.VMEM((2 * per_group, points), f32),
            dma,
            dma((chunks,)),
            dma((chunks, z1)),
            dma((chunks, z1)),
            dma((p1,)),
            dma((p1,)),
            dma((p1,)),
            dma((p1,)),
            dma((p1,)),
            dma((p1,)),
            dma((z1,)),
            dma((z1,)),
            dma((p1,)),
            dma((p1,)),
            dma((z1,)),
            dma((z1,)),
            dma((z1,)),
            dma((z1,)),
        ]
        + [pltpu.VMEM((f_dev * groups, 2, blocks, cw), bf16)] * chunks,
        compiler_params=pltpu.CompilerParams(
            collective_id=0, has_side_effects=True, vmem_limit_bytes=56 * 1024 * 1024
        ),
    )(triads, weights.reshape(1, points), spectra)
    bis, dens, vec, energy, mode = outs
    bis = bis.reshape(pairs_g, 32, 2, 2, 32).transpose(0, 2, 3, 1, 4)
    dens = dens.reshape(f_dev // 2, 32, 2, 2, 32).transpose(0, 2, 3, 1, 4)
    return (
        bis.reshape(per_group, 2, 32, 32),
        dens.reshape(f_dev, 2, 32, 32),
        vec.reshape(per_group, 2, 32),
        energy.reshape(pairs_g, 2, 64)[:, :, 0].reshape(per_group),
        mode.reshape(per_group, 2, points),
    )


def solution(mesh):
    in_specs = (P("freq", None, None, "pts"), P("pts"), P())
    out_specs = (
        P("freq", None, None, None),
        P("freq", None, None, None),
        P("freq", None, None),
        P("freq"),
        P("freq", None, "pts"),
    )
    return jax.shard_map(local, mesh=mesh, in_specs=in_specs, out_specs=out_specs, check_vma=False)
```

time: 426 us -> 238 us (0.56)
  waiting for transfers between devices: 304 us -> 0 us
  Pallas kernels: 0 us -> 224 us
  other arithmetic: 42.4 us -> 2.66 us
  matrix products: 24.8 us -> 0 us
  local copies, waits for them, and re-layouts: 33.8 us -> 10.2 us
  between operations: 14.3 us -> 0.67 us
  starting transfers between devices: 6.52 us -> 0 us
    all_to_all x1 -> x0, waiting for transfers between devices: 245 us -> none  [fetch_slots(): lax.all_to_all(outgoing, 'freq', split_axis=0, concat_axis=0, tiled=True)]
    pallas_call x0 -> x1, Pallas kernels: none -> 224 us  [local(): pl.pallas_call(functools.partial(kernel, groups, point_devs, chunks), out...]
    psum x1 -> x0, waiting for transfers between devices: 58.1 us -> none  [local(): bis_total, dens_total = lax.psum((bis_part, density_part), 'pts')]
    gather x3 -> x0, local copies, waits for them, and re-layouts: 25.5 us -> none  [the longest x1 9.69 us: fetch_slots(): jnp.take(spectra, row_index.reshape(-1), axis=0)]
    dot_general x31 -> x0, matrix products: 24.8 us -> none  [the longest x2 9.33 us: block_gram(): jnp.einsum('tap,tbp->tab', flat_left, flat_right, preferred_element_type=...]
    select_n x5 -> x0, other arithmetic: 20.7 us -> none  [the longest x2 10.9 us: fetch_slots(): jnp.take(spectra, row_index.reshape(-1), axis=0)]
    convert_element_type x2 -> x0, other arithmetic: 11 us -> none  [the longest x1 9.7 us: local(): (spectra.astype(jnp.float32) * weights).astype(jnp.bfloat16)]
    all_to_all x1 -> x0, starting transfers between devices: 6.51 us -> none  [fetch_slots(): lax.all_to_all(outgoing, 'freq', split_axis=0, concat_axis=0, tiled=True)]
  transfers between devices with their start and end apart: 2 -> 0, of which waited for: 2 -> 0; matrix products, arithmetic and copies ran while one was open for 7% -> 0% of each run, Pallas kernels for 0% -> 0%
where the time goes in v1:
time: 238 us; the launch traced here: 237 us
  Pallas kernels  224 us (94%)
  local copies, waits for them, and re-layouts  10.2 us (4%)
  other arithmetic  2.66 us (1%)
    pallas_call x1, Pallas kernels, local(): pl.pallas_call(functools.partial(kernel, groups, point_devs, chunks), out...  224 us

profile of v1, /device:TPU:0, one launch (start us, length us, event | category | flops | bytes accessed | tf_op | source)
XLA Modules:
  0.0 237.4 jit_solution(1344695083747648312)
XLA Ops:
  0.6 1.4 copy.12.tri_ref
  2.0 223.8 %shard_map.74 = (f32[32,8,128]{2,1,0:T(8,128)}, f32[64,8,128]{2,1,0:T(8,128)}, f32[8,1,128]{2,1,0:T(1,128)}, f32[8,1,128]{2,1,0:T(1,128)}, f32[32,2048]{1,0:T(8,128)}) custom-call(s32[64,2]{1,0:T(8,128)} %copy.12.tri_ref, f32[1,2048]{1,0:T(1,128)} %bitcast.9, bf16[32,2,32,2048]{3,2,1,0:T(8,128)(2,1)} %spec_ref.1), custom_call_target="tpu_custom_call" | custom-call | tf_op jit(solution)/shard_map/pallas_call | solution.py:387
  225.8 0.5 broadcast.7
  226.3 1.3 reduce.8
  227.7 0.7 reshape.39
  228.4 1.3 reduce.9
  229.7 0.1 reshape.40
  229.8 0.1 slice_reduce_fusion
  229.9 0.6 reshape_squeeze.3
  230.5 1.8 reshape.37
  232.3 1.1 copy.14
  233.4 1.3 reshape.35
  234.7 0.9 copy.13
  235.6 1.8 reshape.41

commit v2 on v1

--- a/solution.py
+++ b/solution.py
@@ -43,11 +43,95 @@
     return jnp.where(is_real, up, down)
 
 
+def nearest_first(z, groups):
+    table = []
+    for me in range(groups):
+        others = [j for j in range(groups) if j != me]
+        inner = 1 if me < groups // 2 else -1
+        table.append(sorted(others, key=lambda j: (abs(j - me), -(j - me) * inner)))
+    peers = []
+    for s in range(groups - 1):
+        peer = table[0][s] + 0 * z
+        for me in range(1, groups):
+            peer = jnp.where(z == me, table[me][s], peer)
+        peers.append(peer)
+    return peers
+
+
+def plan_kernel(groups, sizes, me_ref, tri_ref, slot_out, order_out, pick_out, need, rank):
+    f_total = need.shape[0]
+    f_dev = f_total // groups
+    triads = tri_ref.shape[0]
+    me = me_ref[0]
+
+    def clear(f, carry):
+        need[f] = 0
+        return carry
+
+    lax.fori_loop(0, f_total, clear, 0, unroll=8)
+
+    def third_of(k, l):
+        return jnp.where(k + l >= f_total, k + l - f_total, k + l)
+
+    def mark(t, carry):
+        k = tri_ref[t, 0]
+        l = tri_ref[t, 1]
+        need[k] = 1
+        need[l] = 1
+        need[third_of(k, l)] = 1
+        return carry
+
+    lax.fori_loop(0, triads, mark, 0, unroll=4)
+
+    def fill(i, carry):
+        order_out[i] = 0
+        return carry
+
+    lax.fori_loop(0, f_dev, fill, 0, unroll=8)
+
+    def own_order(i, count):
+        wanted = need[me * f_dev + i]
+
+        @pl.when(wanted == 1)
+        def _():
+            order_out[count] = i
+
+        return count + wanted
+
+    lax.fori_loop(0, f_dev, own_order, 0, unroll=4)
+
+    most = 0
+    for g in range(groups):
+
+        def count_body(i, count, g=g):
+            rank[g * f_dev + i] = count
+            return count + need[g * f_dev + i]
+
+        most = jnp.maximum(most, lax.fori_loop(0, f_dev, count_body, 0, unroll=8))
+    pick = 0
+    stride = sizes[0]
+    for i in range(len(sizes) - 1):
+        over = most > sizes[i]
+        pick = jnp.where(over, i + 1, pick)
+        stride = jnp.where(over, sizes[i + 1], stride)
+    pick_out[0] = pick
+
+    def slots(t, carry):
+        k = tri_ref[t, 0]
+        l = tri_ref[t, 1]
+        for i, f in enumerate((k, l, third_of(k, l))):
+            slot_out[t, i] = (f // f_dev) * stride + rank[f]
+        return carry
+
+    lax.fori_loop(0, triads, slots, 0, unroll=4)
+
+
 def kernel(
     groups,
     point_devs,
     chunks,
     tri_ref,
+    order_ref,
     w_ref,
     spec_ref,
     bis_out,
@@ -56,6 +140,7 @@
     energy_out,
     mode_out,
     own,
+    stage,
     acc,
     r1,
     s1,
@@ -93,19 +178,20 @@
     z = lax.axis_index("freq")
     q = lax.axis_index("pts")
     f_dev, _, blocks, points = spec_ref.shape
+    rows = stage.shape[0]
     width = points // groups
     cw = width // chunks
     triads = tri_ref.shape[0]
-    f_total = f_dev * groups
     per_group = triads // groups
     pairs_g = per_group // 2
     tpd = fin.shape[0]
     td = dfin.shape[0]
     zs = [lax.rem(z + s, groups) for s in range(1, groups)]
-    zr = [lax.rem(z + groups - s, groups) for s in range(1, groups)]
+    near = nearest_first(z, groups)
     qs = [lax.rem(q + s, point_devs) for s in range(1, point_devs)]
-    qr = [lax.rem(q + point_devs - s, point_devs) for s in range(1, point_devs)]
-
+
+    own_copy = pltpu.make_async_copy(spec_ref, own, own_sem)
+    own_copy.start()
     barrier = pltpu.get_barrier_semaphore()
     for j in zs:
         pl.semaphore_signal(barrier, inc=1, device_id={"freq": j}, device_id_type=MESH)
@@ -115,7 +201,7 @@
 
     def piece(owner, c):
         start = pl.multiple_of(owner * width + c * cw, 128)
-        return spec_ref.at[:, :, :, pl.ds(start, cw)]
+        return stage.at[:, :, :, pl.ds(start, cw)]
 
     def remote(src, dst, send, recv, axis, j):
         return pltpu.make_async_remote_copy(
@@ -127,30 +213,34 @@
             device_id_type=MESH,
         )
 
-    sends = []
-    main = [[None] * (groups - 1) for _ in range(chunks)]
-    for c in range(chunks):
-        for s in range(groups - 1):
+    own_copy.wait()
+
+    def stage_body(i, carry):
+        stage[i] = own[order_ref[i]]
+        return carry
+
+    lax.fori_loop(0, rows, stage_body, 0)
+
+    main = []
+    for s in range(groups - 1):
+        for c in range(chunks):
             copy = remote(
-                piece(zs[s], c),
-                bufs[c].at[pl.ds(z * f_dev, f_dev)],
+                piece(near[s], c),
+                bufs[c].at[pl.ds(z * rows, rows)],
                 main_send.at[c, s],
-                main_recv.at[c, s],
+                main_recv.at[c, z],
                 "freq",
-                zs[s],
+                near[s],
             )
             copy.start()
-            main[c][s] = copy
-    own_copy = pltpu.make_async_copy(spec_ref, own, own_sem)
-    own_copy.start()
+            main.append(copy)
     local_copies = []
     for c in range(chunks):
         copy = pltpu.make_async_copy(
-            piece(z, c), bufs[c].at[pl.ds(z * f_dev, f_dev)], loc_sem.at[c]
+            piece(z, c), bufs[c].at[pl.ds(z * rows, rows)], loc_sem.at[c]
         )
         copy.start()
         local_copies.append(copy)
-    own_copy.wait()
 
     weights_row = w_ref[...]
 
@@ -196,9 +286,9 @@
         local_copies[c].wait()
         for s in range(groups - 1):
             pltpu.make_async_copy(
-                bufs[c].at[pl.ds(zr[s] * f_dev, f_dev)],
-                bufs[c].at[pl.ds(zr[s] * f_dev, f_dev)],
-                main_recv.at[c, s],
+                bufs[c].at[pl.ds(zs[s] * rows, rows)],
+                bufs[c].at[pl.ds(zs[s] * rows, rows)],
+                main_recv.at[c, zs[s]],
             ).wait()
         w_piece = w_ref[:, pl.ds(pl.multiple_of(z * width + c * cw, 128), cw)]
         buf = bufs[c]
@@ -207,12 +297,9 @@
             halves = []
             for h in range(2):
                 t = 2 * i + h
-                k = tri_ref[t, 0]
-                l = tri_ref[t, 1]
-                m = jnp.where(k + l >= f_total, k + l - f_total, k + l)
-                first = buf[k].astype(f32)
-                second = buf[l].astype(f32)
-                third = buf[m]
+                first = buf[tri_ref[t, 0]].astype(f32)
+                second = buf[tri_ref[t, 1]].astype(f32)
+                third = buf[tri_ref[t, 2]]
                 pr = first[0] * second[0] - first[1] * second[1]
                 pi = first[0] * second[1] + first[1] * second[0]
                 pr = (pr * w_piece).astype(bf16)
@@ -227,15 +314,23 @@
                 acc[g, pl.ds(at, 4)] += out
             return carry
 
-        lax.fori_loop(0, triads // 2, triad_body, 0)
+        if c < chunks - 1:
+            lax.fori_loop(0, triads // 2, triad_body, 0)
 
     copies = []
-    for s in range(point_devs - 1):
-        copy = remote(
-            acc.at[:, pl.ds(qs[s] * tpd, tpd)], r1.at[s], r1_send.at[s], r1_recv.at[s], "pts", qs[s]
-        )
-        copy.start()
-        copies.append(copy)
+    for g in range(groups):
+        lax.fori_loop(g * pairs_g, (g + 1) * pairs_g, triad_body, 0)
+        for s in range(point_devs - 1):
+            copy = remote(
+                acc.at[g, pl.ds(qs[s] * tpd, tpd)],
+                r1.at[s, g],
+                r1_send.at[s, g],
+                r1_recv.at[s, g],
+                "pts",
+                qs[s],
+            )
+            copy.start()
+            copies.append(copy)
     for copy in dens_gather:
         copy.wait()
     dens_out[...] = dfull[...]
@@ -320,10 +415,7 @@
         parts = []
         for i in range(4):
             t = g * per_group + j * 4 + i
-            k = tri_ref[t, 0]
-            l = tri_ref[t, 1]
-            m = jnp.where(k + l >= f_total, k + l - f_total, k + l)
-            parts.append(bufs[c][m].reshape(2 * blocks, cw))
+            parts.append(bufs[c][tri_ref[t, 2]].reshape(2 * blocks, cw))
         right = jnp.concatenate(parts, axis=0)
         return jnp.dot(lhs_all[g, j].astype(bf16), right, preferred_element_type=f32)
 
@@ -361,9 +453,8 @@
         return carry
 
     lax.fori_loop(0, per_group // 4, own_mode_body, 0)
-    for c in range(chunks):
-        for s in range(groups - 1):
-            main[c][s].wait_send()
+    for copy in main:
+        copy.wait_send()
     for copy in copies:
         copy.wait()
     mode_out[...] = mode_buf[...]
@@ -384,61 +475,91 @@
     vmem = pl.BlockSpec(memory_space=pltpu.VMEM)
     dma = pltpu.SemaphoreType.DMA
     z1, p1 = groups - 1, point_devs - 1
-    outs = pl.pallas_call(
-        functools.partial(kernel, groups, point_devs, chunks),
+    sizes = sorted({-(-f_dev * n // 32) for n in (25, 26, 27, 28, 29, 32)})
+    smem = pl.BlockSpec(memory_space=pltpu.SMEM)
+    group_index = lax.axis_index("freq").astype(jnp.int32).reshape(1)
+    slots, order, pick = pl.pallas_call(
+        functools.partial(plan_kernel, groups, sizes),
         out_shape=[
-            jax.ShapeDtypeStruct((pairs_g * 4, 8, 128), f32),
-            jax.ShapeDtypeStruct((f_dev * 2, 8, 128), f32),
-            jax.ShapeDtypeStruct((pairs_g, 1, 128), f32),
-            jax.ShapeDtypeStruct((pairs_g, 1, 128), f32),
-            jax.ShapeDtypeStruct((2 * per_group, points), f32),
+            jax.ShapeDtypeStruct((tri_count, 3), jnp.int32),
+            jax.ShapeDtypeStruct((f_dev,), jnp.int32),
+            jax.ShapeDtypeStruct((1,), jnp.int32),
         ],
-        in_specs=[
-            pl.BlockSpec(memory_space=pltpu.SMEM),
-            vmem,
-            pl.BlockSpec(memory_space=pl.ANY),
+        in_specs=[smem, smem],
+        out_specs=[smem] * 3,
+        scratch_shapes=[
+            pltpu.SMEM((f_dev * groups,), jnp.int32),
+            pltpu.SMEM((f_dev * groups,), jnp.int32),
         ],
-        out_specs=[vmem] * 5,
-        scratch_shapes=[
-            pltpu.VMEM(spectra.shape, bf16),
-            pltpu.VMEM((groups, pairs_g * 4, 8, 128), f32),
-            pltpu.VMEM((p1, groups, tpd, 8, 128), f32),
-            pltpu.VMEM((groups, tpd, 8, 128), f32),
-            pltpu.VMEM((z1, tpd, 8, 128), f32),
-            pltpu.VMEM((tpd, 8, 128), f32),
-            pltpu.VMEM((pairs_g * 4, 8, 128), f32),
-            pltpu.VMEM((f_dev * 2, 8, 128), f32),
-            pltpu.VMEM((p1, td, 8, 128), f32),
-            pltpu.VMEM((td, 8, 128), f32),
-            pltpu.VMEM((f_dev * 2, 8, 128), f32),
-            pltpu.VMEM((per_group // 4, 8, 256), f32),
-            pltpu.VMEM((groups, per_group // 4, 8, 256), f32),
-            pltpu.VMEM((groups, 2 * per_group, width), f32),
-            pltpu.VMEM((2 * per_group, points), f32),
-            dma,
-            dma((chunks,)),
-            dma((chunks, z1)),
-            dma((chunks, z1)),
-            dma((p1,)),
-            dma((p1,)),
-            dma((p1,)),
-            dma((p1,)),
-            dma((p1,)),
-            dma((p1,)),
-            dma((z1,)),
-            dma((z1,)),
-            dma((p1,)),
-            dma((p1,)),
-            dma((z1,)),
-            dma((z1,)),
-            dma((z1,)),
-            dma((z1,)),
-        ]
-        + [pltpu.VMEM((f_dev * groups, 2, blocks, cw), bf16)] * chunks,
-        compiler_params=pltpu.CompilerParams(
-            collective_id=0, has_side_effects=True, vmem_limit_bytes=56 * 1024 * 1024
-        ),
-    )(triads, weights.reshape(1, points), spectra)
+    )(group_index, triads)
+
+    def run(branch, rows, slots, order, weights_row, spectra):
+        return pl.pallas_call(
+            functools.partial(kernel, groups, point_devs, chunks),
+            out_shape=[
+                jax.ShapeDtypeStruct((pairs_g * 4, 8, 128), f32),
+                jax.ShapeDtypeStruct((f_dev * 2, 8, 128), f32),
+                jax.ShapeDtypeStruct((pairs_g, 1, 128), f32),
+                jax.ShapeDtypeStruct((pairs_g, 1, 128), f32),
+                jax.ShapeDtypeStruct((2 * per_group, points), f32),
+            ],
+            in_specs=[
+                pl.BlockSpec(memory_space=pltpu.SMEM),
+                pl.BlockSpec(memory_space=pltpu.SMEM),
+                vmem,
+                pl.BlockSpec(memory_space=pl.ANY),
+            ],
+            out_specs=[vmem] * 5,
+            scratch_shapes=[
+                pltpu.VMEM(spectra.shape, bf16),
+                pltpu.VMEM((rows,) + spectra.shape[1:], bf16),
+                pltpu.VMEM((groups, pairs_g * 4, 8, 128), f32),
+                pltpu.VMEM((p1, groups, tpd, 8, 128), f32),
+                pltpu.VMEM((groups, tpd, 8, 128), f32),
+                pltpu.VMEM((z1, tpd, 8, 128), f32),
+                pltpu.VMEM((tpd, 8, 128), f32),
+                pltpu.VMEM((pairs_g * 4, 8, 128), f32),
+                pltpu.VMEM((f_dev * 2, 8, 128), f32),
+                pltpu.VMEM((p1, td, 8, 128), f32),
+                pltpu.VMEM((td, 8, 128), f32),
+                pltpu.VMEM((f_dev * 2, 8, 128), f32),
+                pltpu.VMEM((per_group // 4, 8, 256), f32),
+                pltpu.VMEM((groups, per_group // 4, 8, 256), f32),
+                pltpu.VMEM((groups, 2 * per_group, width), f32),
+                pltpu.VMEM((2 * per_group, points), f32),
+                dma,
+                dma((chunks,)),
+                dma((chunks, z1)),
+                dma((chunks, groups)),
+                dma((p1,)),
+                dma((p1,)),
+                dma((p1,)),
+                dma((p1,)),
+                dma((p1, groups)),
+                dma((p1, groups)),
+                dma((z1,)),
+                dma((z1,)),
+                dma((p1,)),
+                dma((p1,)),
+                dma((z1,)),
+                dma((z1,)),
+                dma((z1,)),
+                dma((z1,)),
+            ]
+            + [pltpu.VMEM((rows * groups, 2, blocks, cw), bf16)] * chunks,
+            compiler_params=pltpu.CompilerParams(
+                collective_id=branch, has_side_effects=True, vmem_limit_bytes=56 * 1024 * 1024
+            ),
+        )(slots, order, weights_row, spectra)
+
+    outs = lax.switch(
+        pick[0],
+        [functools.partial(run, i, n) for i, n in enumerate(sizes)],
+        slots,
+        order,
+        weights.reshape(1, points),
+        spectra,
+    )
     bis, dens, vec, energy, mode = outs
     bis = bis.reshape(pairs_g, 32, 2, 2, 32).transpose(0, 2, 3, 1, 4)
     dens = dens.reshape(f_dev // 2, 32, 2, 2, 32).transpose(0, 2, 3, 1, 4)

time: 238 us -> 209 us (0.88)
  Pallas kernels: 224 us -> 198 us
  local copies, waits for them, and re-layouts: 10.2 us -> 7.45 us
    pallas_call x1 -> x2, Pallas kernels: 224 us -> 198 us  [the longest x1 194 us: run(): pl.pallas_call(functools.partial(kernel, groups, point_devs, chunks), out...]
    pallas_call x2 -> x0, other arithmetic: 2.66 us -> none  [local(): pl.pallas_call(functools.partial(kernel, groups, point_devs, chunks), out...]
where the time goes in v2:
time: 209 us; the launch traced here: 208 us
  Pallas kernels  198 us (95%)
  local copies, waits for them, and re-layouts  7.45 us (4%)
    pallas_call x1, Pallas kernels, run(): pl.pallas_call(functools.partial(kernel, groups, point_devs, chunks), out...  194 us
    pallas_call x1, Pallas kernels, local(): pl.pallas_call(functools.partial(plan_kernel, groups, sizes), out_shape=[...  4.46 us

profile of v2, /device:TPU:0, one launch (start us, length us, event | category | flops | bytes accessed | tf_op | source)
XLA Modules:
  0.0 208.4 jit_solution(10480404750853716451)
XLA Ops:
  0.6 1.4 copy.23.tri_ref
  2.0 4.5 %shard_map.74 = (s32[64,3]{1,0:T(8,128)S(1)}, s32[32]{0:T(128)S(1)}, s32[1]{0:T(128)}) custom-call(s32[1]{0:T(128)} %bitcast.me_ref, s32[64,2]{1,0:T(8,128)} %copy.23.tri_ref), custom_call_target="tpu_custom_call" | custom-call | tf_op jit(solution)/shard_map/pallas_call | solution.py:481
  7.1 193.9 %conditional.1 = ((f32[32,8,128]{2,1,0:T(8,128)S(1)}, f32[64,8,128]{2,1,0:T(8,128)S(1)}, f32[8,1,128]{2,1,0:T(1,128)S(1)}, f32[8,1,128]{2,1,0:T(1,128)S(1)}, f32[32,2048]{1,0:T(8,128)S(1)})) conditional(s32[]{:T(128)} %bitcast.1, (s32[64,3]{1,0:T(8,128)S(1)}, s32[32]{0:T(128)S(1)}, f32[1,2048]{1,0:T(1,128)}, ...), branch_computations={%region_0.0_spmd, %region_1.0_spmd, %region_2.0_spmd, %region_3.0_... | conditional | bytes 8 | solution.py:555
  7.2 193.6 %branch_2_fun.1 = (f32[32,8,128]{2,1,0:T(8,128)S(1)}, f32[64,8,128]{2,1,0:T(8,128)S(1)}, f32[8,1,128]{2,1,0:T(1,128)S(1)}, f32[8,1,128]{2,1,0:T(1,128)S(1)}, f32[32,2048]{1,0:T(8,128)S(1)}) custom-call(s32[64,3]{1,0:T(8,128)S(1)} %get-tuple-element.95.tri_ref, s32[32]{0:T(128)S(1)} %get-tuple-element.96.order_ref, f32[1,2048]{1,0:T(1,128)} %get-tuple-element.97.w_ref, ...), custom_call_target="tpu_custom_call" | custom-call | tf_op jit(solution)/shard_map/cond/branch_2_fun/pallas_call | solution.py:497
  201.0 0.5 broadcast.7
  201.5 0.7 reduce.8
  202.2 0.7 reshape.90
  202.9 0.7 reduce.9
  203.5 0.1 reshape.88
  203.6 0.1 slice_reduce_fusion
  203.7 0.6 reshape_squeeze.17
  204.3 0.8 reshape.65
  205.1 1.1 copy.25
  206.3 0.4 reshape.63
  206.7 0.9 copy.24
  207.6 0.8 reshape.89

commit v3 on v2

--- a/solution.py
+++ b/solution.py
@@ -362,7 +362,6 @@
         copies.append(copy)
     for copy in copies:
         copy.wait()
-    bis_out[...] = full[...]
     mat = full[...].reshape(pairs_g, 32, 128)
 
     lane_m = lane_in((pairs_g, 32, 128))
@@ -419,6 +418,11 @@
         right = jnp.concatenate(parts, axis=0)
         return jnp.dot(lhs_all[g, j].astype(bf16), right, preferred_element_type=f32)
 
+    def two_blocks(g, j, c):
+        pair = [mode_rows(g, 2 * j, c), mode_rows(g, 2 * j + 1, c)]
+        return jnp.concatenate(pair, axis=0).astype(bf16)
+
+    bis_out[...] = full[...]
     for copy in copies:
         copy.wait()
     copies = []
@@ -427,12 +431,12 @@
 
         def mode_body(j, carry, g=g):
             for c in range(chunks):
-                modes[g, pl.ds(pl.multiple_of(j * 8, 8), 8), c * cw : (c + 1) * cw] = mode_rows(
+                modes[g, pl.ds(pl.multiple_of(j * 16, 16), 16), c * cw : (c + 1) * cw] = two_blocks(
                     g, j, c
                 )
             return carry
 
-        lax.fori_loop(0, per_group // 4, mode_body, 0)
+        lax.fori_loop(0, per_group // 8, mode_body, 0)
         copy = remote(
             modes.at[g],
             mode_buf.at[:, pl.ds(pl.multiple_of(z * width, 128), width)],
@@ -447,17 +451,17 @@
     def own_mode_body(j, carry):
         for c in range(chunks):
             mode_buf[
-                pl.ds(pl.multiple_of(j * 8, 8), 8),
+                pl.ds(pl.multiple_of(j * 16, 16), 16),
                 pl.ds(pl.multiple_of(z * width + c * cw, 128), cw),
-            ] = mode_rows(z, j, c)
-        return carry
-
-    lax.fori_loop(0, per_group // 4, own_mode_body, 0)
+            ] = two_blocks(z, j, c)
+        return carry
+
+    lax.fori_loop(0, per_group // 8, own_mode_body, 0)
     for copy in main:
         copy.wait_send()
     for copy in copies:
         copy.wait()
-    mode_out[...] = mode_buf[...]
+    mode_out[...] = mode_buf[...].astype(f32)
 
 
 def local(spectra, weights, triads):
@@ -525,8 +529,8 @@
                 pltpu.VMEM((f_dev * 2, 8, 128), f32),
                 pltpu.VMEM((per_group // 4, 8, 256), f32),
                 pltpu.VMEM((groups, per_group // 4, 8, 256), f32),
-                pltpu.VMEM((groups, 2 * per_group, width), f32),
-                pltpu.VMEM((2 * per_group, points), f32),
+                pltpu.VMEM((groups, 2 * per_group, width), bf16),
+                pltpu.VMEM((2 * per_group, points), bf16),
                 dma,
                 dma((chunks,)),
                 dma((chunks, z1)),

time: 209 us -> 204 us (0.976); the launches traced: 208 us -> 201 us
  Pallas kernels: 198 us -> 190 us
    pallas_call x1, Pallas kernels: 194 us -> 186 us  [run(): pl.pallas_call(functools.partial(kernel, groups, point_devs, chunks), out...]
where the time goes in v3:
time: 204 us; the launch traced here: 201 us
  Pallas kernels  190 us (93%)
  local copies, waits for them, and re-layouts  7.45 us (4%)
    pallas_call x1, Pallas kernels, run(): pl.pallas_call(functools.partial(kernel, groups, point_devs, chunks), out...  186 us
    pallas_call x1, Pallas kernels, local(): pl.pallas_call(functools.partial(plan_kernel, groups, sizes), out_shape=[...  4.46 us

profile of v3, /device:TPU:0, one launch (start us, length us, event | category | flops | bytes accessed | tf_op | source)
XLA Modules:
  0.0 200.7 jit_solution(12240275028146467292)
XLA Ops:
  0.6 1.4 copy.23.tri_ref
  2.0 4.5 %shard_map.74 = (s32[64,3]{1,0:T(8,128)S(1)}, s32[32]{0:T(128)S(1)}, s32[1]{0:T(128)}) custom-call(s32[1]{0:T(128)} %bitcast.me_ref, s32[64,2]{1,0:T(8,128)} %copy.23.tri_ref), custom_call_target="tpu_custom_call" | custom-call | tf_op jit(solution)/shard_map/pallas_call | solution.py:485
  7.1 186.1 %conditional.1 = ((f32[32,8,128]{2,1,0:T(8,128)S(1)}, f32[64,8,128]{2,1,0:T(8,128)S(1)}, f32[8,1,128]{2,1,0:T(1,128)S(1)}, f32[8,1,128]{2,1,0:T(1,128)S(1)}, f32[32,2048]{1,0:T(8,128)S(1)})) conditional(s32[]{:T(128)} %bitcast.1, (s32[64,3]{1,0:T(8,128)S(1)}, s32[32]{0:T(128)S(1)}, f32[1,2048]{1,0:T(1,128)}, ...), branch_computations={%region_0.0_spmd, %region_1.0_spmd, %region_2.0_spmd, %region_3.0_... | conditional | bytes 8 | solution.py:559
  7.2 185.9 %branch_1_fun.1 = (f32[32,8,128]{2,1,0:T(8,128)S(1)}, f32[64,8,128]{2,1,0:T(8,128)S(1)}, f32[8,1,128]{2,1,0:T(1,128)S(1)}, f32[8,1,128]{2,1,0:T(1,128)S(1)}, f32[32,2048]{1,0:T(8,128)S(1)}) custom-call(s32[64,3]{1,0:T(8,128)S(1)} %get-tuple-element.91.tri_ref, s32[32]{0:T(128)S(1)} %get-tuple-element.92.order_ref, f32[1,2048]{1,0:T(1,128)} %get-tuple-element.93.w_ref, ...), custom_call_target="tpu_custom_call" | custom-call | tf_op jit(solution)/shard_map/cond/branch_1_fun/pallas_call | solution.py:501
  193.3 0.5 broadcast.7
  193.8 0.7 reduce.8
  194.4 0.7 reshape.90
  195.1 0.7 reduce.9
  195.8 0.1 reshape.88
  195.9 0.1 slice_reduce_fusion
  196.0 0.6 reshape_squeeze.17
  196.6 0.8 reshape.65
  197.4 1.1 copy.25
  198.5 0.4 reshape.63
  199.0 0.9 copy.24
  199.8 0.8 reshape.89
